TPU v7x, 512 devices: a whole 4x8x8 slice. The times are simulated.
512 devices in a mesh: dp: 16 (over z, core), fsdp: 32 (over x, y).
Axes of the slice: x: 4, y: 8, z: 8, core: 2. Of those that a mesh axis runs over, the one named last changes fastest.
Arguments:
- replica_grads: bfloat16 [16, 8192, 4096], P('dp', 'fsdp'), may hold values from -4 to 4
- slot_table: int32 [32], replicated, may hold values from 0 to 63, as said below
- left_gram_state: float32 [64, 4, 16, 16, 1024], P('fsdp', None, 'dp')
- right_gram_state: float32 [64, 4, 16, 16, 1024], P('fsdp', None, 'dp')
- left_inverse_root: bfloat16 [64, 4, 16, 16, 1024], P('fsdp', None, 'dp')
- right_inverse_root: bfloat16 [64, 4, 16, 16, 1024], P('fsdp', None, 'dp')
Outputs:
- direction: bfloat16 [32, 16, 16, 4096], P('fsdp', 'dp')
- left_new: float32 [64, 4, 16, 16, 1024], P('fsdp', None, 'dp')
- right_new: float32 [64, 4, 16, 16, 1024], P('fsdp', None, 'dp')
Inputs may be any that keep to these rules, and one draw needn't show every extreme that they name: `slot_table`: the entries are distinct; slot v belongs to owner v // 2 of the flat shards' devices; some owner holds 2 blocks.
All inputs are finite; a program needn't handle non-finite values.
Results may differ from a plain program's by a relative error of at most 0.02.
Values may be sent and summed in bfloat16 or wider, within the bound.
No kernel may reach another device: no remote copies, remote signals or barrier semaphores. Data moves between devices by JAX's collectives and lax.ppermute only.
A program may use at most 128 MiB of HBM per device.

v0:
```python
import jax
import jax.numpy as jnp
from jax import lax
from jax.sharding import PartitionSpec as P


def on_device(
    replica_grads,
    slot_table,
    left_gram_state,
    right_gram_state,
    left_inverse_root,
    right_inverse_root,
):
    slots_here = left_gram_state.shape[0]
    sub_blocks = left_gram_state.shape[1]
    strip_rows = left_gram_state.shape[3]
    block_size = left_gram_state.shape[4]
    band_rows = replica_grads.shape[1]
    model_width = replica_grads.shape[2]
    per_band = model_width // block_size
    shards = lax.axis_size("fsdp")
    groups = lax.axis_size("dp")
    total_slots = shards * slots_here
    block_count = slot_table.shape[0]
    band_index = lax.axis_index("fsdp")
    strip_index = lax.axis_index("dp")
    slot_indices = jnp.arange(total_slots, dtype=jnp.int32)
    right_entire = lax.all_gather(right_inverse_root, "dp", axis=2, tiled=True).reshape(
        slots_here, block_size, block_size
    )
    summed = lax.psum_scatter(
        replica_grads[0].astype(jnp.float32).astype(jnp.bfloat16),
        "dp",
        scatter_dimension=0,
        tiled=True,
    )
    row_block = band_index * band_rows // block_size
    targets = lax.dynamic_slice_in_dim(slot_table, row_block * per_band, per_band, 0)
    chooser = (targets[:, None] == slot_indices[None, :]).astype(jnp.bfloat16)
    own_slots = band_index * slots_here + jnp.arange(slots_here, dtype=jnp.int32)
    holder = slot_table[None, :] == own_slots[:, None]
    block_of = jnp.sum(
        jnp.where(holder, jnp.arange(block_count, dtype=jnp.int32)[None, :], 0), axis=1
    )
    first_band = block_of // per_band * sub_blocks
    outgoing = jnp.einsum(
        "cn,tcb->ntb",
        chooser,
        summed.reshape(strip_rows, per_band, block_size),
        preferred_element_type=jnp.float32,
    ).astype(jnp.bfloat16)
    outgoing = outgoing.reshape(shards, slots_here, strip_rows, block_size)
    arrived = lax.all_to_all(outgoing, "fsdp", split_axis=0, concat_axis=0, tiled=True)
    owned_rows = jax.vmap(
        lambda portion, offset: lax.dynamic_slice_in_dim(portion, offset, sub_blocks, 0),
        in_axes=(1, 0),
    )(arrived, first_band)
    owned_rows = owned_rows.reshape(slots_here, sub_blocks, 1, strip_rows, block_size)
    entire = lax.all_gather(owned_rows, "dp", axis=2, tiled=True).reshape(
        slots_here, block_size, block_size
    )
    my_rows = owned_rows.reshape(slots_here, sub_blocks * strip_rows, block_size)
    left_gram = jnp.einsum("mrc,mnc->mrn", my_rows, entire, preferred_element_type=jnp.float32)
    left_new = left_gram_state + (left_gram / block_size).reshape(left_gram_state.shape)
    my_columns = lax.dynamic_index_in_dim(
        entire.reshape(slots_here, block_size, sub_blocks, groups, strip_rows),
        strip_index,
        3,
        keepdims=False,
    )
    my_columns = my_columns.reshape(slots_here, block_size, sub_blocks * strip_rows)
    right_gram = jnp.einsum("mnr,mnc->mrc", my_columns, entire, preferred_element_type=jnp.float32)
    right_new = right_gram_state + (right_gram / block_size).reshape(right_gram_state.shape)
    left_rows = left_inverse_root.reshape(slots_here, sub_blocks * strip_rows, block_size)
    mixed_rows = jnp.einsum(
        "mrn,mnc->mrc", left_rows, entire, preferred_element_type=jnp.float32
    ).astype(jnp.bfloat16)
    result = jnp.einsum(
        "mrn,mnc->mrc", mixed_rows, right_entire, preferred_element_type=jnp.float32
    )
    outcome = result.astype(jnp.bfloat16).reshape(slots_here, sub_blocks, strip_rows, block_size)
    homeward = jax.vmap(
        lambda portion, offset: lax.dynamic_update_slice_in_dim(
            jnp.zeros((shards, strip_rows, block_size), jnp.bfloat16), portion, offset, 0
        ),
        out_axes=1,
    )(outcome, first_band)
    returned = lax.all_to_all(homeward, "fsdp", split_axis=0, concat_axis=0, tiled=True)
    picked = jnp.einsum(
        "cn,ntb->tcb",
        chooser,
        returned.reshape(total_slots, strip_rows, block_size),
        preferred_element_type=jnp.float32,
    ).astype(jnp.bfloat16)
    direction = picked.reshape(1, 1, strip_rows, model_width)
    return (direction, left_new, right_new)


def solution(mesh):
    placed = (
        P("dp", "fsdp", None),
        P(),
        P("fsdp", None, "dp", None, None),
        P("fsdp", None, "dp", None, None),
        P("fsdp", None, "dp", None, None),
        P("fsdp", None, "dp", None, None),
    )
    return jax.shard_map(
        on_device,
        mesh=mesh,
        in_specs=placed,
        out_specs=(
            P("fsdp", "dp", None, None),
            P("fsdp", None, "dp", None, None),
            P("fsdp", None, "dp", None, None),
        ),
        check_vma=False,
    )
```

profile of v0, /device:TPU:16, one launch (start us, length us, event | category | flops | bytes accessed | tf_op | source)
XLA Modules:
  0.0 276.2 jit_solution(1561728517146626942)
XLA Ops:
  7.2 0.7 reduce-scatter.2.cloned.1.call-update
  8.0 0.7 all-gather.4.cloned.1.call-update
  8.7 0.7 dynamic_slice.7
  9.4 69.5 %reduce-scatter.2.cloned.1.call-done = bf16[16,4096]{1,0:T(8,128)(2,1)} async-done(((bf16[256,4096]{1,0:T(8,128)(2,1)}), bf16[16,4096]{1,0:T(8,128)(2,1)}) %reduce-scatter.2.cloned.1.call-update) | async-done | bytes 131088 | tf_op jit(solution)/shard_map/reduce_scatter | solution.py:32
  78.9 1.0 reshape.110
  79.9 0.8 convolution_convert_fusion
  80.7 2.5 copy.35
  83.2 9.8 %all-to-all-start = ((bf16[32,2,16,1024]{3,2,1,0:T(8,128)(2,1)}), bf16[32,2,16,1024]{3,2,1,0:T(8,128)(2,1)S(1)}, u32[]{:S(2)}, u32[]{:S(2)}) async-start(bf16[32,2,16,1024]{3,2,1,0:T(8,128)(2,1)} %bitcast.3), calls=%async_computation.1 | async-start | bytes 4194304 | tf_op jit(solution)/shard_map/all_to_all | solution.py:54
  93.3 45.8 %all-to-all-done = bf16[32,2,16,1024]{3,2,1,0:T(8,128)(2,1)S(1)} async-done(((bf16[32,2,16,1024]{3,2,1,0:T(8,128)(2,1)}), bf16[32,2,16,1024]{3,2,1,0:T(8,128)(2,1)S(1)}, u32[]{:S(2)}, u32[]{:S(2)}) %all-to-all-start) | async-done | bytes 2097184 | tf_op jit(solution)/shard_map/all_to_all | solution.py:54
  139.1 1.3 gather_fusion
  140.6 42.7 %all-gather.6.cloned.1.call-done = bf16[2,4,256,1024]{3,2,1,0:T(8,128)(2,1)} async-done(((bf16[2,4,16,1024]{3,2,1,0:T(8,128)(2,1)}), bf16[2,4,256,1024]{3,2,1,0:T(8,128)(2,1)}) %all-gather.6.cloned.1.call-update) | async-done | bytes 4194320 | tf_op jit(solution)/shard_map/all_gather | solution.py:60
  183.4 5.1 %convolution_convert_fusion.2 = bf16[2,64,1024]{2,1,0:T(8,128)(2,1)S(1)} fusion(bf16[2,1024,1024]{2,1,0:T(8,128)(2,1)} %bitcast.80, bf16[2,64,1024]{2,1,0:T(8,128)(2,1)S(1)} %bitcast.75, bf16[2,1024,1024]{2,1,0:T(8,128)(2,1)} %bitcast.76), kind=kOutput, calls=%fused_computation.12 | convolution fusion | flops 537133056 | bytes 8912896 | tf_op jit(solution)/shard_map/mrn,mnc->mrc/dot_general | solution.py:79
  188.4 1.6 broadcast_in_dim.16.clone
  190.0 17.4 %while.1 = (s32[]{:T(128)}, bf16[2,32,16,1024]{3,2,0,1:T(8,128)(2,1)}, s32[2,4]{1,0:T(2,128)S(1)}, bf16[2,4,16,1024]{3,2,1,0:T(8,128)(2,1)S(1)}, s32[]{:T(128)}, /*index=5*/s32[4]{0:T(128)S(1)}) while((s32[]{:T(128)}, bf16[2,32,16,1024]{3,2,0,1:T(8,128)(2,1)}, s32[2,4]{1,0:T(2,128)S(1)}, bf16[2,4,16,1024]{3,2,1,0:T(8,128)(2,1)S(1)}, s32[]{:T(128)}, ...), condition=%wide.while_cond, body=%wide.while_body.sunk | while | flops 65565 | bytes 657586 | solution.py:84
  190.7 3.3 %and_reduce_fusion.2 = pred[]{:T(512)} fusion(s32[4]{0:T(128)S(1)} %get-tuple-element.91, s32[1]{0:T(128)} %bitcast.71, s32[1]{0:T(128)} %bitcast.72, s32[1]{0:T(128)} %bitcast.73, s32[1]{0:T(128)} %bitcast.74), kind=kLoop, calls=%fused_computation.3.clone.1 | loop fusion | flops 27 | bytes 33 | tf_op jit(solution)/shard_map/vmap(vmap())/scatter
  194.0 2.2 constant_dynamic-slice_fusion.6
  196.2 2.6 bitcast_dynamic-update-slice_fusion.2
  198.8 0.7 fusion.24
  199.4 3.3 %and_reduce_fusion.2 = pred[]{:T(512)} fusion(s32[4]{0:T(128)S(1)} %get-tuple-element.91, s32[1]{0:T(128)} %bitcast.71, s32[1]{0:T(128)} %bitcast.72, s32[1]{0:T(128)} %bitcast.73, s32[1]{0:T(128)} %bitcast.74), kind=kLoop, calls=%fused_computation.3.clone.1 | loop fusion | flops 27 | bytes 33 | tf_op jit(solution)/shard_map/vmap(vmap())/scatter
  202.7 2.2 constant_dynamic-slice_fusion.6
  204.9 2.6 bitcast_dynamic-update-slice_fusion.2
  207.5 9.8 %all-to-all-start.1 = ((bf16[32,2,16,1024]{3,2,1,0:T(8,128)(2,1)}), bf16[32,2,16,1024]{3,2,1,0:T(8,128)(2,1)S(1)}, u32[]{:S(2)}, u32[]{:S(2)}) async-start(bf16[32,2,16,1024]{3,2,1,0:T(8,128)(2,1)} %bitcast.10), calls=%async_computation.2 | async-start | bytes 4194304 | tf_op jit(solution)/shard_map/all_to_all | solution.py:89
  217.3 7.5 %copy.33 = bf16[2,4,256,1024]{2,1,3,0:T(4,128)(2,1)} copy(bf16[2,4,256,1024]{3,2,1,0:T(8,128)(2,1)} %all-gather.6.cloned.1.call-done) | data formatting | bytes 8388608 | tf_op jit(solution)/shard_map/all_gather | solution.py:60
  224.8 7.7 %reshape_reshape.7 = bf16[2,1024,4,16,16]{1,4,3,2,0:T(8,128)(2,1)} reshape(bf16[2,4,256,1024]{2,1,3,0:T(4,128)(2,1)} %copy.33) | data formatting | bytes 8388608 | tf_op jit(solution)/shard_map/reshape;reshape | solution.py:67
  232.6 1.1 constant_dynamic-slice_fusion.2
  233.7 3.5 %convolution_multiply_fusion = f32[2,64,1024]{2,1,0:T(8,128)S(1)} fusion(bf16[2,1024,64]{1,2,0:T(8,128)(2,1)S(1)} %bitcast.84, bf16[2,1024,1024]{2,1,0:T(8,128)(2,1)} %bitcast.77), kind=kOutput, calls=%fused_computation.9 | convolution fusion | flops 268566528 | bytes 4980736 | tf_op jit(solution)/shard_map/mnr,mnc->mrc/dot_general | solution.py:73
  237.2 0.9 add.53
  238.1 1.4 convolution_multiply_fusion.1
  239.5 0.9 add.51
  240.3 27.4 %all-to-all-done.1 = bf16[32,2,16,1024]{3,2,1,0:T(8,128)(2,1)S(1)} async-done(((bf16[32,2,16,1024]{3,2,1,0:T(8,128)(2,1)}), bf16[32,2,16,1024]{3,2,1,0:T(8,128)(2,1)S(1)}, u32[]{:S(2)}, u32[]{:S(2)}) %all-to-all-start.1) | async-done | bytes 2097184 | tf_op jit(solution)/shard_map/all_to_all | solution.py:89
  267.7 1.2 fusion.5
  268.9 0.7 reshape.118
  (31 shorter events, 1.2 us)
Async XLA Ops:
  7.2 176.2 %copy-start = (bf16[2,4,1,16,1024]{4,3,2,1,0:T(8,128)(2,1)S(1)}, bf16[2,4,1,16,1024]{4,3,2,1,0:T(8,128)(2,1)}, u32[]{:S(2)}) copy-start(bf16[2,4,1,16,1024]{4,3,2,1,0:T(8,128)(2,1)} %param.10) | copy-start | bytes 786436
  7.2 71.7 %reduce-scatter.2.cloned.1.call-start = ((), (), s32[]{:S(2)}) async-start(), calls=%async_computation.3 | async-start | bytes 2228224 | tf_op jit(solution)/shard_map/reduce_scatter | solution.py:32
  7.9 132.7 %all-gather.4.cloned.1.call-start = ((), (), s32[]{:S(2)}) async-start(), calls=%async_computation.4 | async-start | bytes 4456448 | tf_op jit(solution)/shard_map/all_gather | solution.py:29
  80.7 12.4 %copy-start.7 = (s32[32]{0:T(128)S(1)}, s32[32]{0:T(128)}, u32[]{:S(2)}) copy-start(s32[32]{0:T(128)} %param.7) | copy-start | bytes 388
  80.7 59.7 %copy-start.6 = (s32[3]{0:T(128)S(1)}, s32[3]{0:T(128)}, u32[]{:S(2)}) copy-start(s32[3]{0:T(128)} %constant.55.clone.1) | copy-start | bytes 40
  83.2 55.9 %all-to-all-start = ((bf16[32,2,16,1024]{3,2,1,0:T(8,128)(2,1)}), bf16[32,2,16,1024]{3,2,1,0:T(8,128)(2,1)S(1)}, u32[]{:S(2)}, u32[]{:S(2)}) async-start(bf16[32,2,16,1024]{3,2,1,0:T(8,128)(2,1)} %bitcast.3), calls=%async_computation.1 | async-start | bytes 4194304 | tf_op jit(solution)/shard_map/all_to_all | solution.py:54
  93.1 90.3 %all-gather.6.cloned.1.call-start = ((), (), s32[]{:S(2)}) async-start(), calls=%async_computation.5 | async-start | bytes 4456448 | tf_op jit(solution)/shard_map/all_gather | solution.py:60
  183.4 6.7 %copy-start.5 = (s32[4]{0:T(128)S(1)}, s32[4]{0:T(128)}, u32[]{:S(2)}) copy-start(s32[4]{0:T(128)} %constant.139) | copy-start | bytes 52
  207.5 60.3 %all-to-all-start.1 = ((bf16[32,2,16,1024]{3,2,1,0:T(8,128)(2,1)}), bf16[32,2,16,1024]{3,2,1,0:T(8,128)(2,1)S(1)}, u32[]{:S(2)}, u32[]{:S(2)}) async-start(bf16[32,2,16,1024]{3,2,1,0:T(8,128)(2,1)} %bitcast.10), calls=%async_computation.2 | async-start | bytes 4194304 | tf_op jit(solution)/shard_map/all_to_all | solution.py:89
  232.6 4.6 %copy-start.3 = (f32[2,4,1,16,1024]{4,3,2,1,0:T(8,128)S(1)}, f32[2,4,1,16,1024]{4,3,2,1,0:T(8,128)}, u32[]{:S(2)}) copy-start(f32[2,4,1,16,1024]{4,3,2,1,0:T(8,128)} %param.9) | copy-start | bytes 1572868
  232.6 5.5 %copy-start.1 = (bf16[2,4,256,1024]{3,2,1,0:T(8,128)(2,1)S(1)}, bf16[2,4,256,1024]{3,2,1,0:T(8,128)(2,1)}, u32[]{:S(2)}) copy-start(bf16[2,4,256,1024]{3,2,1,0:T(8,128)(2,1)} %all-gather.6.cloned.1.call-done) | copy-start | bytes 12582916
  232.6 5.5 %copy-start.2 = (bf16[2,4,16,1024]{3,2,1,0:T(8,128)(2,1)S(1)}, bf16[2,4,16,1024]{3,2,1,0:T(8,128)(2,1)}, u32[]{:S(2)}) copy-start(bf16[2,4,16,1024]{3,2,1,0:T(8,128)(2,1)} %gather_fusion) | copy-start | bytes 786436
  237.2 2.3 copy-start.4
Sparse Core Ops, SparseCore 0:
  10.8 68.0 reduce-scatter.1
  81.0 42.9 all-gather.3
  140.6 42.7 all-gather.5
where the time goes:
time: 277 us; the launch traced here: 276 us
  waiting for transfers between devices  187 us (68%)
  local copies, waits for them, and re-layouts  30.1 us (11%)
  starting transfers between devices  19.8 us (7%)
  between operations  13.9 us (5%)
  other arithmetic  13.7 us (5%)
  matrix products  12 us (4%)
    reduce_scatter x1, waiting for transfers between devices, on_device(): lax.psum_scatter(replica_grads[0].astype(jnp.float32).astype(jnp.bfloat16...  69.5 us
    all_to_all x1, waiting for transfers between devices, on_device(): lax.all_to_all(outgoing, 'fsdp', split_axis=0, concat_axis=0, tiled=True)  45.8 us
    all_gather x1, waiting for transfers between devices, on_device(): lax.all_gather(owned_rows, 'dp', axis=2, tiled=True)  42.7 us
    all_to_all x1, waiting for transfers between devices, on_device(): lax.all_to_all(homeward, 'fsdp', split_axis=0, concat_axis=0, tiled=True)  27.4 us
    scatter x4, other arithmetic  11.7 us
    all_to_all x1, starting transfers between devices, on_device(): lax.all_to_all(outgoing, 'fsdp', split_axis=0, concat_axis=0, tiled=True)  9.83 us
    all_to_all x1, starting transfers between devices, on_device(): lax.all_to_all(homeward, 'fsdp', split_axis=0, concat_axis=0, tiled=True)  9.82 us
    another operation x1, local copies, waits for them, and re-layouts, on_device(): entire.reshape(slots_here, block_size, sub_blocks, groups, strip_rows)  7.75 us
  transfers between devices with their start and end apart: 5, of which 4 were waited for; matrix products, arithmetic and copies ran while one was open for 11% of the time, Pallas kernels for 0%

commit v1 on v0

--- a/solution.py
+++ b/solution.py
@@ -57,9 +57,9 @@
         in_axes=(1, 0),
     )(arrived, first_band)
     owned_rows = owned_rows.reshape(slots_here, sub_blocks, 1, strip_rows, block_size)
-    entire = lax.all_gather(owned_rows, "dp", axis=2, tiled=True).reshape(
-        slots_here, block_size, block_size
-    )
+    entire = jnp.concatenate(
+        lax.all_to_all(jnp.stack([owned_rows] * lax.axis_size("dp")), "dp", 0, 0), axis=2
+    ).reshape(slots_here, block_size, block_size)
     my_rows = owned_rows.reshape(slots_here, sub_blocks * strip_rows, block_size)
     left_gram = jnp.einsum("mrc,mnc->mrn", my_rows, entire, preferred_element_type=jnp.float32)
     left_new = left_gram_state + (left_gram / block_size).reshape(left_gram_state.shape)

time: 277 us -> 365 us (1.32)
  the two profiles are of different devices: /device:TPU:16 before, /device:TPU:2 now
where the time goes in v1:
time: 365 us; the launch traced here: 364 us
  waiting for transfers between devices  230 us (63%)
  local copies, waits for them, and re-layouts  70 us (19%)
  starting transfers between devices  24.6 us (7%)
  between operations  14.2 us (4%)
  other arithmetic  13.6 us (4%)
  matrix products  11.7 us (3%)
    all_to_all x1, waiting for transfers between devices, on_device(): lax.all_to_all(jnp.stack([owned_rows] * lax.axis_size('dp')), 'dp', 0, 0)  113 us
    reduce_scatter x1, waiting for transfers between devices, on_device(): lax.psum_scatter(replica_grads[0].astype(jnp.float32).astype(jnp.bfloat16...  70.4 us
    all_to_all x1, waiting for transfers between devices, on_device(): lax.all_to_all(outgoing, 'fsdp', split_axis=0, concat_axis=0, tiled=True)  45 us
    another operation x1, local copies, waits for them, and re-layouts, on_device(): entire.reshape(slots_here, block_size, sub_blocks, groups, strip_rows)  31.8 us
    dynamic_slice x2, local copies, waits for them, and re-layouts, on_device(): lax.dynamic_index_in_dim(entire.reshape(slots_here, block_size, sub_block...  17.7 us
    scatter x4, other arithmetic  11.5 us
    all_to_all x1, starting transfers between devices, on_device(): lax.all_to_all(outgoing, 'fsdp', split_axis=0, concat_axis=0, tiled=True)  9.86 us
    all_to_all x1, starting transfers between devices, on_device(): lax.all_to_all(homeward, 'fsdp', split_axis=0, concat_axis=0, tiled=True)  8.16 us
  transfers between devices with their start and end apart: 5, of which 3 were waited for; matrix products, arithmetic and copies ran while one was open for 17% of the time, Pallas kernels for 0%

profile of v1, /device:TPU:2, one launch (start us, length us, event | category | flops | bytes accessed | tf_op | source)
XLA Modules:
  0.0 363.8 jit_solution(12298872263226894064)
XLA Ops:
  7.2 0.7 reduce-scatter.2.cloned.1.call-update
  7.9 0.7 dynamic_slice.7
  8.7 70.4 %reduce-scatter.2.cloned.1.call-done = bf16[16,4096]{1,0:T(8,128)(2,1)} async-done(((bf16[256,4096]{1,0:T(8,128)(2,1)}), bf16[16,4096]{1,0:T(8,128)(2,1)}) %reduce-scatter.2.cloned.1.call-update) | async-done | bytes 131088 | tf_op jit(solution)/shard_map/reduce_scatter | solution.py:32
  79.1 1.0 reshape.109
  80.1 0.8 convolution_convert_fusion
  80.9 2.5 copy.39
  83.4 9.9 %all-to-all-start = ((bf16[32,2,16,1024]{3,2,1,0:T(8,128)(2,1)}), bf16[32,2,16,1024]{3,2,1,0:T(8,128)(2,1)S(1)}, u32[]{:S(2)}, u32[]{:S(2)}) async-start(bf16[32,2,16,1024]{3,2,1,0:T(8,128)(2,1)} %bitcast.3), calls=%async_computation.1 | async-start | bytes 4194304 | tf_op jit(solution)/shard_map/all_to_all | solution.py:54
  93.5 45.0 %all-to-all-done = bf16[32,2,16,1024]{3,2,1,0:T(8,128)(2,1)S(1)} async-done(((bf16[32,2,16,1024]{3,2,1,0:T(8,128)(2,1)}), bf16[32,2,16,1024]{3,2,1,0:T(8,128)(2,1)S(1)}, u32[]{:S(2)}, u32[]{:S(2)}) %all-to-all-start) | async-done | bytes 2097184 | tf_op jit(solution)/shard_map/all_to_all | solution.py:54
  139.0 2.5 stack.3
  141.5 6.5 %all-to-all-start.1 = ((bf16[16,2,4,1,16,1024]{5,4,2,1,3,0:T(8,128)(2,1)}), bf16[16,2,4,1,16,1024]{5,4,2,1,3,0:T(8,128)(2,1)}, u32[]{:S(2)}, u32[]{:S(2)}) async-start(bf16[16,2,4,1,16,1024]{5,4,2,1,3,0:T(8,128)(2,1)} %stack.3), calls=%async_computation.2 | async-start | bytes 8388608 | tf_op jit(solution)/shard_map/all_to_all | solution.py:61
  148.0 0.7 all-gather.2.cloned.1.call-update
  148.9 113.0 %all-to-all-done.1 = bf16[16,2,4,1,16,1024]{5,4,2,1,3,0:T(8,128)(2,1)} async-done(((bf16[16,2,4,1,16,1024]{5,4,2,1,3,0:T(8,128)(2,1)}), bf16[16,2,4,1,16,1024]{5,4,2,1,3,0:T(8,128)(2,1)}, u32[]{:S(2)}, u32[]{:S(2)}) %all-to-all-start.1) | async-done | bytes 4194336 | tf_op jit(solution)/shard_map/all_to_all | solution.py:61
  261.9 5.1 %copy.31 = bf16[2,4,16,1,16,1024]{5,4,2,1,0,3:T(8,128)(2,1)} copy(bf16[2,4,16,1,16,1024]{5,4,1,0,3,2:T(8,128)(2,1)} %bitcast.6) | data formatting | bytes 8388608 | tf_op jit(solution)/shard_map/reshape | solution.py:60
  267.0 5.1 %convolution_convert_fusion.2 = bf16[2,64,1024]{2,1,0:T(8,128)(2,1)S(1)} fusion(bf16[2,1024,1024]{2,1,0:T(8,128)(2,1)} %bitcast.83, bf16[2,64,1024]{2,1,0:T(8,128)(2,1)S(1)} %bitcast.78, bf16[2,1024,1024]{2,1,0:T(8,128)(2,1)} %bitcast.79), kind=kOutput, calls=%fused_computation.12 | convolution fusion | flops 537133056 | bytes 8912896 | tf_op jit(solution)/shard_map/mrn,mnc->mrc/dot_general | solution.py:79
  272.1 1.6 broadcast_in_dim.16.clone
  273.8 17.2 %while.1 = (s32[]{:T(128)}, bf16[2,32,16,1024]{3,2,0,1:T(8,128)(2,1)}, s32[2,4]{1,0:T(2,128)S(1)}, bf16[2,4,16,1024]{3,2,1,0:T(8,128)(2,1)S(1)}, s32[]{:T(128)}, /*index=5*/s32[4]{0:T(128)S(1)}) while((s32[]{:T(128)}, bf16[2,32,16,1024]{3,2,0,1:T(8,128)(2,1)}, s32[2,4]{1,0:T(2,128)S(1)}, bf16[2,4,16,1024]{3,2,1,0:T(8,128)(2,1)S(1)}, s32[]{:T(128)}, ...), condition=%wide.while_cond, body=%wide.while_body.sunk | while | flops 65565 | bytes 657586 | solution.py:84
  274.4 3.2 and_reduce_fusion.2
  277.6 2.2 constant_dynamic-slice_fusion.6
  279.8 2.5 bitcast_dynamic-update-slice_fusion.2
  283.0 3.2 and_reduce_fusion.2
  286.2 2.2 constant_dynamic-slice_fusion.6
  288.4 2.5 bitcast_dynamic-update-slice_fusion.2
  290.9 8.2 %all-to-all-start.2 = ((bf16[32,2,16,1024]{3,2,1,0:T(8,128)(2,1)}), bf16[32,2,16,1024]{3,2,1,0:T(8,128)(2,1)S(1)}, u32[]{:S(2)}, u32[]{:S(2)}) async-start(bf16[32,2,16,1024]{3,2,1,0:T(8,128)(2,1)} %bitcast.11), calls=%async_computation.3 | async-start | bytes 4194304 | tf_op jit(solution)/shard_map/all_to_all | solution.py:89
  299.1 31.8 %reshape_reshape_reshape.3 = bf16[2,1024,4,16,16]{4,3,2,1,0:T(8,128)(2,1)} reshape(bf16[2,4,16,1,16,1024]{5,4,2,1,0,3:T(8,128)(2,1)} %copy.31) | data formatting | bytes 8388608 | tf_op jit(solution)/shard_map/reshape;reshape;reshape | solution.py:67
  330.9 9.0 %constant_dynamic-slice_fusion.2 = bf16[2,1024,4,1,16]{4,3,2,1,0:T(2,128)(2,1)} fusion(bf16[2,1024,4,16,16]{4,3,2,1,0:T(8,128)(2,1)} %reshape_reshape_reshape.3, s32[]{:T(128)S(6)} %select_n.44), kind=kLoop, calls=%fused_computation.31 | loop fusion | bytes 524292 | tf_op jit(solution)/shard_map/jit(dynamic_index_in_dim)/dynamic_slice | solution.py:66
  340.0 8.7 %copy.37 = bf16[2,1024,4,1,16]{1,4,2,0,3:T(8,128)(2,1)S(1)} copy(bf16[2,1024,4,1,16]{4,3,2,1,0:T(2,128)(2,1)} %constant_dynamic-slice_fusion.2) | data formatting | bytes 524288 | tf_op jit(solution)/shard_map/jit(dynamic_index_in_dim)/dynamic_slice | solution.py:66
  348.6 3.2 convolution_multiply_fusion
  351.8 0.9 add.53
  352.7 1.4 convolution_multiply_fusion.1
  354.1 0.9 add.51
  355.0 1.2 fusion.5
  356.2 0.7 reshape.116
  (32 shorter events, 2.3 us)
Async XLA Ops:
  7.2 259.9 %copy-start = (bf16[2,4,1,16,1024]{4,3,2,1,0:T(8,128)(2,1)S(1)}, bf16[2,4,1,16,1024]{4,3,2,1,0:T(8,128)(2,1)}, u32[]{:S(2)}) copy-start(bf16[2,4,1,16,1024]{4,3,2,1,0:T(8,128)(2,1)} %param.10) | copy-start | bytes 786436
  7.2 71.9 %reduce-scatter.2.cloned.1.call-start = ((), (), s32[]{:S(2)}) async-start(), calls=%async_computation.4 | async-start | bytes 2228224 | tf_op jit(solution)/shard_map/reduce_scatter | solution.py:32
  80.9 12.4 %copy-start.7 = (s32[32]{0:T(128)S(1)}, s32[32]{0:T(128)}, u32[]{:S(2)}) copy-start(s32[32]{0:T(128)} %param.7) | copy-start | bytes 388
  83.4 55.1 %all-to-all-start = ((bf16[32,2,16,1024]{3,2,1,0:T(8,128)(2,1)}), bf16[32,2,16,1024]{3,2,1,0:T(8,128)(2,1)S(1)}, u32[]{:S(2)}, u32[]{:S(2)}) async-start(bf16[32,2,16,1024]{3,2,1,0:T(8,128)(2,1)} %bitcast.3), calls=%async_computation.1 | async-start | bytes 4194304 | tf_op jit(solution)/shard_map/all_to_all | solution.py:54
  141.5 7.2 %copy-start.6 = (s32[3]{0:T(128)S(1)}, s32[3]{0:T(128)}, u32[]{:S(2)}) copy-start(s32[3]{0:T(128)} %constant.55.clone.1) | copy-start | bytes 40
  141.5 120.4 %all-to-all-start.1 = ((bf16[16,2,4,1,16,1024]{5,4,2,1,3,0:T(8,128)(2,1)}), bf16[16,2,4,1,16,1024]{5,4,2,1,3,0:T(8,128)(2,1)}, u32[]{:S(2)}, u32[]{:S(2)}) async-start(bf16[16,2,4,1,16,1024]{5,4,2,1,3,0:T(8,128)(2,1)} %stack.3), calls=%async_computation.2 | async-start | bytes 8388608 | tf_op jit(solution)/shard_map/all_to_all | solution.py:61
  148.0 119.0 %all-gather.2.cloned.1.call-start = ((), (), s32[]{:S(2)}) async-start(), calls=%async_computation.5 | async-start | bytes 4456448 | tf_op jit(solution)/shard_map/all_gather | solution.py:29
  267.0 6.7 %copy-start.5 = (s32[4]{0:T(128)S(1)}, s32[4]{0:T(128)}, u32[]{:S(2)}) copy-start(s32[4]{0:T(128)} %constant.139) | copy-start | bytes 52
  290.9 64.0 %all-to-all-start.2 = ((bf16[32,2,16,1024]{3,2,1,0:T(8,128)(2,1)}), bf16[32,2,16,1024]{3,2,1,0:T(8,128)(2,1)S(1)}, u32[]{:S(2)}, u32[]{:S(2)}) async-start(bf16[32,2,16,1024]{3,2,1,0:T(8,128)(2,1)} %bitcast.11), calls=%async_computation.3 | async-start | bytes 4194304 | tf_op jit(solution)/shard_map/all_to_all | solution.py:89
  340.0 11.9 %copy-start.3 = (f32[2,4,1,16,1024]{4,3,2,1,0:T(8,128)S(1)}, f32[2,4,1,16,1024]{4,3,2,1,0:T(8,128)}, u32[]{:S(2)}) copy-start(f32[2,4,1,16,1024]{4,3,2,1,0:T(8,128)} %param.9) | copy-start | bytes 1572868
  348.6 4.1 %copy-start.2 = (bf16[2,4,16,1,16,1024]{5,4,2,1,0,3:T(8,128)(2,1)S(1)}, bf16[2,4,16,1,16,1024]{5,4,2,1,0,3:T(8,128)(2,1)}, u32[]{:S(2)}) copy-start(bf16[2,4,16,1,16,1024]{5,4,2,1,0,3:T(8,128)(2,1)} %copy.31) | copy-start | bytes 12582916
  351.8 2.3 copy-start.4
  352.7 4.2 %copy-start.1 = (bf16[2,4,1,16,1024]{4,3,2,1,0:T(8,128)(2,1)S(1)}, bf16[2,4,1,16,1024]{4,3,2,1,0:T(8,128)(2,1)}, u32[]{:S(2)}) copy-start(bf16[2,4,1,16,1024]{4,3,2,1,0:T(8,128)(2,1)} %param.10) | copy-start | bytes 786436
Sparse Core Ops, SparseCore 0:
  10.8 68.2 reduce-scatter.1
  151.0 97.5 all-gather.1
